TPU v7x, 128 devices: a 2x2x16 block of a 8x8x16 slice. The times are simulated.
128 devices in a mesh: groups: 4 (over x, y), freq: 16 (over z), mgrp: 2 (over core).
Axes of the slice: x: 2, y: 2, z: 16, core: 2. Of those that a mesh axis runs over, the one named last changes fastest.
The devices are a block of a 8x8x16 slice.
Arguments:
- seeds: int32 [128, 1024], P('groups', 'mgrp'), parts along dimension 0, may hold values from 0 to 1073741823
- noise_amp: float32 [1024, 512], P(('groups', 'freq')), parts along dimension 0, may hold values from 0.3 to 3
- singular_projection: bfloat16 [128, 256, 16, 512], P('groups', 'freq'), parts along dimension 0, may hold values from -0.25 to 0.25
- kl_vecs: bfloat16 [128, 1536, 4096], P(('groups', 'freq'), 'mgrp'), parts along dimension 0, may hold values from -0.09375 to 0.09375
- m_order: int32 [128], P('groups'), parts along dimension 0, may hold values from 0 to 31, each once
- mode_counts: int32 [128], P('groups'), parts along dimension 0, may hold values from 384 to 1536, as said below
Outputs:
- kl_coeffs: bfloat16 [128, 1536, 1024], P(('groups', 'freq'), None, 'mgrp'), parts along dimension 0
There are 4 independent parts, one for each index of `groups`. A program takes and returns all parts, laid end to end along the dimension named above; each array names one. Nothing has to cross between parts.
Inputs may be any that keep to these rules, and one draw needn't show every extreme that they name: `m_order`: each m appears in exactly one slot. `mode_counts`: some m keeps all 1536 modes.
All inputs are finite; a program needn't handle non-finite values.
Results may differ from a plain program's by a relative error of at most 0.0058.
Values may be sent and summed in bfloat16 or wider, within the bound.
A program may use at most 192 MiB of HBM per device.

v0:
```python
import jax
import jax.numpy as jnp
from jax import lax
from jax.sharding import PartitionSpec as P

golden = 1640531527


def scramble(hashed_seed):
    hashed_seed = hashed_seed ^ hashed_seed >> 16 & 65535
    hashed_seed = hashed_seed * 2146121005
    hashed_seed = hashed_seed ^ hashed_seed >> 15 & 131071
    hashed_seed = hashed_seed * 1863026059
    hashed_seed = hashed_seed ^ hashed_seed >> 16 & 65535
    return ((hashed_seed & 65535).astype(jnp.float32) - 32767.5) / 18918.0


def per_device(seeds, noise_amp, singular_projection, kl_vecs, m_order, mode_counts):
    freq_count = lax.axis_size("freq")
    freq_index = lax.axis_index("freq")
    local_chan = singular_projection.shape[1]
    modes_chan = singular_projection.shape[2]
    baseline_pairs = singular_projection.shape[3]
    batch_groups = kl_vecs.shape[0]
    half_reals = seeds.shape[1]
    order_grid = m_order.reshape(freq_count, batch_groups)
    global_channel = freq_index * local_chan + jnp.arange(local_chan, dtype=jnp.int32)
    channel_index = (
        global_channel[:, None] * baseline_pairs
        + jnp.arange(baseline_pairs, dtype=jnp.int32)[None, :]
    )
    every_m = jnp.arange(m_order.shape[0], dtype=jnp.int32)

    def project(m_number):
        weights = lax.dynamic_index_in_dim(singular_projection, m_number, 0, keepdims=False)
        seed_row = lax.dynamic_index_in_dim(seeds, m_number, 0, keepdims=False)
        noise_draw = scramble(seed_row[None, None, :] + channel_index[:, :, None] * golden)
        visible = (noise_amp[:, :, None] * noise_draw).astype(jnp.bfloat16)
        stacked = jnp.einsum("fkb,fbr->fkr", weights, visible, preferred_element_type=jnp.float32)
        return stacked.astype(jnp.bfloat16).reshape(local_chan * modes_chan, half_reals)

    outputs = []
    for batch_index in range(batch_groups):
        m_numbers = order_grid[:, batch_index]
        grouped = lax.map(jax.vmap(project), m_numbers.reshape(-1, 4))
        outgoing = grouped.reshape(m_numbers.shape[0], local_chan * modes_chan, half_reals)
        arrived = lax.all_to_all(outgoing, "freq", split_axis=0, concat_axis=1, tiled=True)
        vectors = arrived[0]
        position_index = freq_index * batch_groups + batch_index
        kept_m_number = jnp.sum(jnp.where(every_m == position_index, m_order, 0))
        kept_limit = jnp.sum(jnp.where(every_m == kept_m_number, mode_counts, 0))
        eigen_panel = kl_vecs[batch_index]
        coeffs = jnp.dot(
            lax.all_gather(eigen_panel, "mgrp", axis=0, tiled=True),
            vectors,
            preferred_element_type=jnp.float32,
        )
        row_index = jnp.arange(coeffs.shape[0], dtype=jnp.int32)
        outputs.append(jnp.where(row_index[:, None] < kept_limit, coeffs, 0.0).astype(jnp.bfloat16))
    return jnp.stack(outputs, 0)


def solution(mesh):
    placed = (
        P("groups", "mgrp"),
        P(("groups", "freq"), None),
        P("groups", "freq", None, None),
        P(("groups", "freq"), "mgrp", None),
        P("groups"),
        P("groups"),
    )
    return jax.shard_map(
        per_device,
        mesh=mesh,
        in_specs=placed,
        out_specs=P(("groups", "freq"), None, "mgrp"),
        check_vma=False,
    )
```

profile of v0, /device:TPU:69, one launch (start us, length us, event | category | flops | bytes accessed | tf_op | source)
XLA Modules:
  0.0 576.0 jit_solution(3924146653526477834)
XLA Ops:
  6.5 0.7 reshape.125
  7.3 0.7 slice_reduce_fusion.1
  8.0 0.1 reshape_squeeze.7
  8.1 2.4 broadcast.237.clone
  10.4 152.2 %while.27 = (s32[]{:T(128)}, bf16[4,4,256,512]{3,2,1,0:T(8,128)(2,1)}, s32[4,4]{1,0:T(4,128)S(1)}, bf16[32,16,16,512]{3,2,1,0:T(8,128)(2,1)}, s32[32,512]{1,0:T(...) while((s32[]{:T(128)}, bf16[4,4,256,512]{3,2,1,0:T(8,128)(2,1)}, ...), condition=%wide.region_7.8_spmd.clone, body=%wide.region_6.7_spmd.clone.sunk | while | flops 822632448 | bytes 6480165 | solution.py:45
  10.5 4.0 gather_fusion.2
  14.5 1.4 gather_fusion.3
  15.9 0.8 broadcast_multiply_fusion.5
  16.7 30.7 %fusion.82 = bf16[4,16,16,512]{3,2,1,0:T(8,128)(2,1)S(1)} fusion(bf16[4,16,16,512]{3,2,1,0:T(8,128)(2,1)S(1)} %gather_fusion.2, s32[4,512]{1,0:T(4,128)S(1)} %gather_fusion.3, f32[16,512]{1,0:T(8,128)S(1)} %broadcast_multiply_fusion.5, s32[16,512]{1,0:T(8,128)S(1)} %add_multiply_fusion.6), kind=kOutput, calls=%fused_computation.41.clone.1 | convolution fusion | flops 822607872 | bytes 2170880 | tf_op jit(solution)/shard_map/while/body/eval_jaxpr/vmap(fkb,fbr->fkr)/dot_general | solution.py:39
  47.4 1.1 constant_dynamic-update-slice_fusion.5
  48.5 4.0 gather_fusion.2
  52.5 1.4 gather_fusion.3
  54.0 0.8 broadcast_multiply_fusion.5
  54.7 0.1 add_multiply_fusion.6
  54.8 30.7 %fusion.82 = bf16[4,16,16,512]{3,2,1,0:T(8,128)(2,1)S(1)} fusion(bf16[4,16,16,512]{3,2,1,0:T(8,128)(2,1)S(1)} %gather_fusion.2, s32[4,512]{1,0:T(4,128)S(1)} %gather_fusion.3, f32[16,512]{1,0:T(8,128)S(1)} %broadcast_multiply_fusion.5, s32[16,512]{1,0:T(8,128)S(1)} %add_multiply_fusion.6), kind=kOutput, calls=%fused_computation.41.clone.1 | convolution fusion | flops 822607872 | bytes 2170880 | tf_op jit(solution)/shard_map/while/body/eval_jaxpr/vmap(fkb,fbr->fkr)/dot_general | solution.py:39
  85.5 1.1 constant_dynamic-update-slice_fusion.5
  86.5 4.0 gather_fusion.2
  90.6 1.4 gather_fusion.3
  92.0 0.8 broadcast_multiply_fusion.5
  92.8 30.7 %fusion.82 = bf16[4,16,16,512]{3,2,1,0:T(8,128)(2,1)S(1)} fusion(bf16[4,16,16,512]{3,2,1,0:T(8,128)(2,1)S(1)} %gather_fusion.2, s32[4,512]{1,0:T(4,128)S(1)} %gather_fusion.3, f32[16,512]{1,0:T(8,128)S(1)} %broadcast_multiply_fusion.5, s32[16,512]{1,0:T(8,128)S(1)} %add_multiply_fusion.6), kind=kOutput, calls=%fused_computation.41.clone.1 | convolution fusion | flops 822607872 | bytes 2170880 | tf_op jit(solution)/shard_map/while/body/eval_jaxpr/vmap(fkb,fbr->fkr)/dot_general | solution.py:39
  123.5 1.1 constant_dynamic-update-slice_fusion.5
  124.6 4.0 gather_fusion.2
  128.6 1.4 gather_fusion.3
  130.0 0.8 broadcast_multiply_fusion.5
  130.9 30.7 %fusion.82 = bf16[4,16,16,512]{3,2,1,0:T(8,128)(2,1)S(1)} fusion(bf16[4,16,16,512]{3,2,1,0:T(8,128)(2,1)S(1)} %gather_fusion.2, s32[4,512]{1,0:T(4,128)S(1)} %gather_fusion.3, f32[16,512]{1,0:T(8,128)S(1)} %broadcast_multiply_fusion.5, s32[16,512]{1,0:T(8,128)S(1)} %add_multiply_fusion.6), kind=kOutput, calls=%fused_computation.41.clone.1 | convolution fusion | flops 822607872 | bytes 2170880 | tf_op jit(solution)/shard_map/while/body/eval_jaxpr/vmap(fkb,fbr->fkr)/dot_general | solution.py:39
  161.6 1.1 constant_dynamic-update-slice_fusion.5
  162.6 17.6 %all-to-all-start.1 = ((bf16[16,256,512]{2,1,0:T(8,128)(2,1)}), bf16[16,256,512]{2,1,0:T(8,128)(2,1)}, u32[]{:S(2)}, u32[]{:S(2)}) async-start(bf16[16,256,512]{2,1,0:T(8,128)(2,1)} %bitcast.63), calls=%async_computation.1 | async-start | bytes 8388608 | tf_op jit(solution)/shard_map/all_to_all | solution.py:47
  180.3 10.5 %fusion.66 = (bf16[1,768,4096]{2,1,0:T(8,128)(2,1)}, bf16[1,768,4096]{2,1,0:T(8,128)(2,1)}) fusion(bf16[2,768,4096]{2,1,0:T(8,128)(2,1)} %param.13), kind=kLoop, calls=%fused_computation.80 | loop fusion | bytes 25165824 | tf_op jit(solution)/shard_map/slice | solution.py:52
  190.8 0.1 reshape_squeeze.6
  190.9 2.3 broadcast.237.clone.1
  193.3 145.7 %while.26 = (s32[]{:T(128)}, bf16[4,4,256,512]{3,2,1,0:T(8,128)(2,1)}, s32[4,4]{1,0:T(4,128)S(1)}, bf16[32,16,16,512]{3,2,1,0:T(8,128)(2,1)}, s32[32,512]{1,0:T(...) while((s32[]{:T(128)}, bf16[4,4,256,512]{3,2,1,0:T(8,128)(2,1)}, ...), condition=%wide.region_3.4_spmd.clone, body=%wide.region_2.3_spmd.clone.sunk | while | flops 822632448 | bytes 6480165 | solution.py:45
  193.3 4.0 gather_fusion
  197.3 0.6 gather_fusion.1
  197.9 0.1 add_multiply_fusion.5
  197.9 30.7 %fusion.79 = bf16[4,16,16,512]{3,2,1,0:T(8,128)(2,1)S(1)} fusion(bf16[4,16,16,512]{3,2,1,0:T(8,128)(2,1)S(1)} %gather_fusion, s32[4,512]{1,0:T(4,128)S(1)} %gather_fusion.1, f32[16,512]{1,0:T(8,128)S(1)} %broadcast_multiply_fusion.4, s32[16,512]{1,0:T(8,128)S(1)} %add_multiply_fusion.5), kind=kOutput, calls=%fused_computation.16.clone.1 | convolution fusion | flops 822607872 | bytes 2170880 | tf_op jit(solution)/shard_map/while/body/eval_jaxpr/vmap(fkb,fbr->fkr)/dot_general | solution.py:39
  228.6 1.0 constant_dynamic-update-slice_fusion.4
  229.7 4.0 gather_fusion
  233.7 0.6 gather_fusion.1
  234.3 0.1 add_multiply_fusion.5
  234.4 30.7 %fusion.79 = bf16[4,16,16,512]{3,2,1,0:T(8,128)(2,1)S(1)} fusion(bf16[4,16,16,512]{3,2,1,0:T(8,128)(2,1)S(1)} %gather_fusion, s32[4,512]{1,0:T(4,128)S(1)} %gather_fusion.1, f32[16,512]{1,0:T(8,128)S(1)} %broadcast_multiply_fusion.4, s32[16,512]{1,0:T(8,128)S(1)} %add_multiply_fusion.5), kind=kOutput, calls=%fused_computation.16.clone.1 | convolution fusion | flops 822607872 | bytes 2170880 | tf_op jit(solution)/shard_map/while/body/eval_jaxpr/vmap(fkb,fbr->fkr)/dot_general | solution.py:39
  265.0 1.1 constant_dynamic-update-slice_fusion.4
  266.1 4.0 gather_fusion
  270.1 0.6 gather_fusion.1
  270.7 0.1 add_multiply_fusion.5
  270.8 30.7 %fusion.79 = bf16[4,16,16,512]{3,2,1,0:T(8,128)(2,1)S(1)} fusion(bf16[4,16,16,512]{3,2,1,0:T(8,128)(2,1)S(1)} %gather_fusion, s32[4,512]{1,0:T(4,128)S(1)} %gather_fusion.1, f32[16,512]{1,0:T(8,128)S(1)} %broadcast_multiply_fusion.4, s32[16,512]{1,0:T(8,128)S(1)} %add_multiply_fusion.5), kind=kOutput, calls=%fused_computation.16.clone.1 | convolution fusion | flops 822607872 | bytes 2170880 | tf_op jit(solution)/shard_map/while/body/eval_jaxpr/vmap(fkb,fbr->fkr)/dot_general | solution.py:39
  301.5 1.1 constant_dynamic-update-slice_fusion.4
  302.6 4.0 gather_fusion
  306.6 0.6 gather_fusion.1
  307.2 0.1 add_multiply_fusion.5
  307.3 30.7 %fusion.79 = bf16[4,16,16,512]{3,2,1,0:T(8,128)(2,1)S(1)} fusion(bf16[4,16,16,512]{3,2,1,0:T(8,128)(2,1)S(1)} %gather_fusion, s32[4,512]{1,0:T(4,128)S(1)} %gather_fusion.1, f32[16,512]{1,0:T(8,128)S(1)} %broadcast_multiply_fusion.4, s32[16,512]{1,0:T(8,128)S(1)} %add_multiply_fusion.5), kind=kOutput, calls=%fused_computation.16.clone.1 | convolution fusion | flops 822607872 | bytes 2170880 | tf_op jit(solution)/shard_map/while/body/eval_jaxpr/vmap(fkb,fbr->fkr)/dot_general | solution.py:39
  337.9 1.1 constant_dynamic-update-slice_fusion.4
  339.0 22.9 %all-to-all-done.1 = bf16[16,256,512]{2,1,0:T(8,128)(2,1)} async-done(((bf16[16,256,512]{2,1,0:T(8,128)(2,1)}), bf16[16,256,512]{2,1,0:T(8,128)(2,1)}, u32[]{:S(2)}, u32[]{:S(2)}) %all-to-all-start.1) | async-done | bytes 4194336 | tf_op jit(solution)/shard_map/all_to_all | solution.py:47
  361.9 11.3 %all-to-all-start = ((bf16[16,256,512]{2,1,0:T(8,128)(2,1)}), bf16[16,256,512]{2,1,0:T(8,128)(2,1)}, u32[]{:S(2)}, u32[]{:S(2)}) async-start(bf16[16,256,512]{2,1,0:T(8,128)(2,1)} %bitcast.62), calls=%async_computation | async-start | bytes 8388608 | tf_op jit(solution)/shard_map/all_to_all | solution.py:47
  373.2 0.2 all-gather.5.cloned.1.call-start
  373.5 0.6 all-gather.5.cloned.1.call-update
  374.0 0.6 fusion.62
  374.7 1.9 fusion.63
  376.6 1.2 iota_compare_fusion
  377.9 11.8 %fusion.59 = bf16[1,1536,512]{1,2,0:T(8,128)(2,1)} fusion(bf16[4096,512]{1,0:T(8,128)(2,1)} %bitcast.6, bf16[1,1536,4096]{2,1,0:T(8,128)(2,1)} %all-gather.7.cloned.1.call-done, pred[1536]{0:T(1024)(128)(4,1)S(1)} %get-tuple-element.255), kind=kOutput, calls=%fused_computation.66 | convolution fusion | flops 6444023808 | bytes 18351616 | tf_op jit(solution)/shard_map/dot_general | solution.py:53
  389.7 20.2 %all-gather.5.cloned.1.call-done = bf16[1,1536,4096]{2,1,0:T(8,128)(2,1)} async-done(((bf16[1,768,4096]{2,1,0:T(8,128)(2,1)}), bf16[1,1536,4096]{2,1,0:T(8,128)(2,1)}) %all-gather.5.cloned.1.call-update) | async-done | bytes 12582928 | tf_op jit(solution)/shard_map/all_gather | solution.py:54
  409.9 145.0 %all-to-all-done = bf16[16,256,512]{2,1,0:T(8,128)(2,1)} async-done(((bf16[16,256,512]{2,1,0:T(8,128)(2,1)}), bf16[16,256,512]{2,1,0:T(8,128)(2,1)}, u32[]{:S(2)}, u32[]{:S(2)}) %all-to-all-start) | async-done | bytes 4194336 | tf_op jit(solution)/shard_map/all_to_all | solution.py:47
  554.9 11.1 %fusion.56 = bf16[1,1536,512]{1,2,0:T(8,128)(2,1)S(1)} fusion(bf16[4096,512]{1,0:T(8,128)(2,1)} %bitcast.1, bf16[1,1536,4096]{2,1,0:T(8,128)(2,1)} %all-gather.5.cloned.1.call-done, pred[1536]{0:T(1024)(128)(4,1)S(1)} %get-tuple-element.256), kind=kOutput, calls=%fused_computation.65 | convolution fusion | flops 6444023808 | bytes 18351616 | tf_op jit(solution)/shard_map/dot_general | solution.py:53
  566.0 0.3 pad_maximum_fusion
  566.3 2.8 copy.8
  (31 shorter events, 0.5 us)
Async XLA Ops:
  162.6 199.3 %all-to-all-start.1 = ((bf16[16,256,512]{2,1,0:T(8,128)(2,1)}), bf16[16,256,512]{2,1,0:T(8,128)(2,1)}, u32[]{:S(2)}, u32[]{:S(2)}) async-start(bf16[16,256,512]{2,1,0:T(8,128)(2,1)} %bitcast.63), calls=%async_computation.1 | async-start | bytes 8388608 | tf_op jit(solution)/shard_map/all_to_all | solution.py:47
  180.2 10.6 %copy-start.4 = (s32[16]{0:T(128)S(1)}, s32[16]{0:T(128)}, u32[]{:S(2)}) copy-start(s32[16]{0:T(128)} %get-tuple-element.219) | copy-start | bytes 196
  180.2 13.1 %copy-start = (s32[32,512]{1,0:T(8,128)S(1)}, s32[32,512]{1,0:T(8,128)}, u32[]{:S(2)}) copy-start(s32[32,512]{1,0:T(8,128)} %get-tuple-element.402) | copy-start | bytes 196612
  180.2 13.0 %copy-start.1 = (f32[16,512]{1,0:T(8,128)S(1)}, f32[16,512]{1,0:T(8,128)}, u32[]{:S(2)}) copy-start(f32[16,512]{1,0:T(8,128)} %get-tuple-element.403) | copy-start | bytes 98308
  180.2 197.6 %all-gather.7.cloned.1.call-start = ((), (), s32[]{:S(2)}) async-start(), calls=%async_computation.3 | async-start | bytes 18874368 | tf_op jit(solution)/shard_map/all_gather | solution.py:54
  339.0 35.0 %copy-start.3 = (s32[32]{0:T(128)S(1)}, s32[32]{0:T(128)}, u32[]{:S(2)}) copy-start(s32[32]{0:T(128)} %param.14) | copy-start | bytes 388
  339.0 35.7 %copy-start.5 = (s32[32]{0:T(128)S(1)}, s32[32]{0:T(128)}, u32[]{:S(2)}) copy-start(s32[32]{0:T(128)} %param.15) | copy-start | bytes 388
  361.9 193.0 %all-to-all-start = ((bf16[16,256,512]{2,1,0:T(8,128)(2,1)}), bf16[16,256,512]{2,1,0:T(8,128)(2,1)}, u32[]{:S(2)}, u32[]{:S(2)}) async-start(bf16[16,256,512]{2,1,0:T(8,128)(2,1)} %bitcast.62), calls=%async_computation | async-start | bytes 8388608 | tf_op jit(solution)/shard_map/all_to_all | solution.py:47
  373.2 36.7 %all-gather.5.cloned.1.call-start = ((), (), s32[]{:S(2)}) async-start(), calls=%async_computation.2 | async-start | bytes 18874368 | tf_op jit(solution)/shard_map/all_gather | solution.py:54
  554.9 11.1 %copy-start.2 = (bf16[1,1536,512]{1,2,0:T(8,128)(2,1)S(1)}, bf16[1,1536,512]{1,2,0:T(8,128)(2,1)}, u32[]{:S(2)}) copy-start(bf16[1,1536,512]{1,2,0:T(8,128)(2,1)} %fusion.59) | copy-start | bytes 4718596
Sparse Core Ops, SparseCore 0:
  191.0 34.2 all-gather.6
  375.7 34.1 all-gather.4
where the time goes:
time: 577 us; the launch traced here: 576 us
  matrix products  268 us (46%)
  waiting for transfers between devices  189 us (33%)
  local copies, waits for them, and re-layouts  68.1 us (12%)
  starting transfers between devices  29.2 us (5%)
  between operations  13.5 us (2%)
  other arithmetic  7.8 us (1%)
    dot_general x8, matrix products, project(): jnp.einsum('fkb,fbr->fkr', weights, visible, preferred_element_type=jnp.f...  245 us
    all_to_all x2, waiting for transfers between devices, per_device(): lax.all_to_all(outgoing, 'freq', split_axis=0, concat_axis=1, tiled=True)  168 us
    gather x8, local copies, waits for them, and re-layouts, project(): lax.dynamic_index_in_dim(singular_projection, m_number, 0, keepdims=False)  32 us
    all_to_all x2, starting transfers between devices, per_device(): lax.all_to_all(outgoing, 'freq', split_axis=0, concat_axis=1, tiled=True)  28.9 us
    dot_general x2, matrix products, per_device(): jnp.dot(lax.all_gather(eigen_panel, 'mgrp', axis=0, tiled=True), vectors,...  22.9 us
    all_gather x2, waiting for transfers between devices, per_device(): lax.all_gather(eigen_panel, 'mgrp', axis=0, tiled=True)  20.2 us
  transfers between devices with their start and end apart: 4, of which 3 were waited for; matrix products, arithmetic and copies ran while one was open for 30% of the time, Pallas kernels for 0%

commit v1 on v0

v1 whole, which is shorter than its diff:
```python
import functools
import math

import jax
import jax.numpy as jnp
from jax import lax
from jax.experimental import pallas as pl
from jax.experimental.pallas import tpu as pltpu
from jax.sharding import PartitionSpec as P

GOLDEN = 1640531527
MIX_A = 2146121005
MIX_B = 1863026059
MESH = pl.DeviceIdType.MESH
LANES = 128
ROWS = 128
NT = (((1,), (1,)), ((), ()))


def wrap(value):
    return (value + 2**31) % 2**32 - 2**31


def draw(x):
    x = x ^ lax.shift_right_logical(x, 16)
    x = x * MIX_A
    x = x ^ lax.shift_right_logical(x, 15)
    x = x * MIX_B
    x = x ^ lax.shift_right_logical(x, 16)
    return ((x & 65535).astype(jnp.float32) - 32767.5).astype(jnp.bfloat16)


def weigh_kernel(picked, projection, amp, out):
    del picked
    out[0] = (projection[0].astype(jnp.float32) * amp[...]).astype(jnp.bfloat16)


def weigh(picked, projection, amp):
    count = picked.shape[0]
    block = (1,) + projection.shape[1:]
    return pl.pallas_call(
        weigh_kernel,
        out_shape=jax.ShapeDtypeStruct((count,) + projection.shape[1:], jnp.bfloat16),
        grid_spec=pltpu.PrefetchScalarGridSpec(
            num_scalar_prefetch=1,
            grid=(count,),
            in_specs=[
                pl.BlockSpec(block, lambda d, picked: (picked[d], 0, 0, 0)),
                pl.BlockSpec(amp.shape, lambda d, picked: (0, 0, 0)),
            ],
            out_specs=pl.BlockSpec(block, lambda d, picked: (d, 0, 0, 0)),
        ),
        name="weigh",
    )(picked, projection, amp)


def project_kernel(
    size, base_ref, weights_ref, kl_ref, out_ref,
    base, wide, weights, kl, svd, coef, own, other,
    base_sem, weights_send, weights_recv, kl_own, kl_send, kl_recv, out_own, out_send, out_recv,
):
    z = lax.axis_index("freq")
    c = lax.axis_index("mgrp")
    partner = {"mgrp": 1 - c}
    channels, modes, entries = weights.shape[1:]
    reals = base.shape[0]
    half = reals // 2
    deep = channels * modes
    kept = kl.shape[1]
    share = kept // 2
    per_trip = LANES // modes
    trips = channels // per_trip
    slab = kept // trips

    def distance(j):
        return (j % 2) * ((j + 1) // 2) + (1 - j % 2) * ((size - j // 2) % size)

    def source(j):
        return (z - distance(j) + size) % size

    barrier = pltpu.get_barrier_semaphore()
    pl.semaphore_signal(barrier, inc=1, device_id=partner, device_id_type=MESH)
    for d in range(1, size):
        pl.semaphore_signal(barrier, inc=1, device_id={"freq": (z + d) % size}, device_id_type=MESH)

    own_weights = pltpu.make_async_copy(weights_ref.at[0], weights.at[0], weights_recv.at[0])
    own_weights.start()
    own_base = pltpu.make_async_copy(base_ref.at[0], base.at[pl.ds(0, half)], base_sem.at[0])
    own_base.start()
    kl[size] = jnp.zeros(kl.shape[1:], kl.dtype)
    svd[...] = jnp.zeros(svd.shape, svd.dtype)
    coef[...] = jnp.zeros(coef.shape, coef.dtype)
    pl.semaphore_wait(barrier, size)

    far_base = pltpu.make_async_remote_copy(
        src_ref=base_ref.at[1], dst_ref=base.at[pl.ds(half, half)], send_sem=base_sem.at[1], recv_sem=base_sem.at[2],
        device_id=partner, device_id_type=MESH,
    )
    far_base.start()

    def send_weights(d):
        return pltpu.make_async_remote_copy(
            src_ref=weights_ref.at[d], dst_ref=weights.at[d], send_sem=weights_send.at[d], recv_sem=weights_recv.at[d],
            device_id={"freq": (z + d) % size}, device_id_type=MESH,
        )

    def local_panel(tile):
        return pltpu.make_async_copy(
            kl_ref.at[c, :, pl.ds(pl.multiple_of(tile * deep, deep), deep)],
            kl.at[tile, pl.ds(pl.multiple_of(c * share, share), share)],
            kl_own.at[tile],
        )

    def send_panel(tile):
        return pltpu.make_async_remote_copy(
            src_ref=kl_ref.at[1 - c, :, pl.ds(pl.multiple_of(tile * deep, deep), deep)],
            dst_ref=kl.at[tile, pl.ds(pl.multiple_of(c * share, share), share)],
            send_sem=kl_send.at[tile], recv_sem=kl_recv.at[tile],
            device_id=partner, device_id_type=MESH,
        )

    @pl.loop(1, size)
    def _(j):
        send_weights(distance(j)).start()

    @pl.loop(0, size)
    def _(j):
        local_panel(source(j)).start()
        send_panel(source(j)).start()

    own_base.wait()
    far_base.wait()
    for b in range(entries // LANES):
        wide[:, b * LANES:(b + 1) * LANES] = base[...] + wrap(b * LANES * GOLDEN)

    @pl.loop(0, size)
    def _(j):
        cur = j % 2
        prev = 1 - cur
        at = distance(j)

        @pl.when(j == 0)
        def _():
            own_weights.wait()

        @pl.when(j > 0)
        def _():
            send_weights(at).wait_recv()
            local_panel(source(j - 1)).wait()
            send_panel(source(j - 1)).wait_recv()

        first = jnp.minimum(j, 1)
        tile = (1 - first) * size + first * source(jnp.maximum(j - 1, 0))
        start = source(j) * channels

        @pl.loop(0, trips)
        def _(t):
            rows = []
            for u in range(per_trip):
                before = [jnp.zeros((u * modes, entries), jnp.bfloat16)] if u else []
                after = [jnp.zeros((LANES - (u + 1) * modes, entries), jnp.bfloat16)] if u + 1 < per_trip else []
                rows.append(jnp.concatenate(before + [weights[at, t * per_trip + u]] + after, 0))
            stacked = jnp.concatenate(rows, 1)
            top = pl.multiple_of(t * slab, slab)
            blocks = reals // ROWS
            wide_n = 2 * ROWS
            for r in range(blocks):
                here = slice(r * ROWS, (r + 1) * ROWS)
                if r % 2 == 0:
                    there = slice(r * ROWS, r * ROWS + wide_n)
                    coef[pl.ds(top, slab), there] += lax.dot_general(
                        kl[tile, pl.ds(top, slab), :], svd[prev, there, :], NT, preferred_element_type=jnp.float32
                    )
                visible = jnp.concatenate(
                    [
                        draw(wide[here, :] + (start + t * per_trip + u) * wrap(entries * GOLDEN))
                        for u in range(per_trip)
                    ],
                    1,
                )
                projected = lax.dot_general(visible, stacked, NT, preferred_element_type=jnp.float32)
                svd[cur, here, pl.ds(pl.multiple_of(t * LANES, LANES), LANES)] = projected.astype(jnp.bfloat16)

    local_panel(source(size - 1)).wait()
    send_panel(source(size - 1)).wait_recv()

    parts = out_own.shape[0]
    piece = kept // parts

    def keep(i):
        return pltpu.make_async_copy(
            own.at[pl.ds(i * piece, piece)], out_ref.at[c, pl.ds(i * piece, piece)], out_own.at[i]
        )

    def hand(i):
        return pltpu.make_async_remote_copy(
            src_ref=other.at[pl.ds(i * piece, piece)], dst_ref=out_ref.at[c, pl.ds(i * piece, piece)],
            send_sem=out_send.at[i], recv_sem=out_recv.at[i], device_id=partner, device_id_type=MESH,
        )

    last = source(size - 1)
    for i in range(parts):
        here = slice(i * piece, (i + 1) * piece)
        for side, target in ((0, own), (1, other)):
            there = slice(side * half, (side + 1) * half)
            target[here, :] = (
                coef[here, there]
                + lax.dot_general(
                    kl[last, here, :], svd[(size - 1) % 2, there, :], NT, preferred_element_type=jnp.float32
                )
            ).astype(jnp.bfloat16)
        if i:
            keep(i - 1).start()
            hand(i - 1).start()
    keep(parts - 1).start()
    hand(parts - 1).start()

    @pl.loop(1, size)
    def _(d):
        send_weights(d).wait_send()

    @pl.loop(0, size)
    def _(tile):
        send_panel(tile).wait_send()

    for i in range(parts):
        keep(i).wait()
        hand(i).wait()


def project(size, base, weights, kl_vecs, reals):
    slots, share, length = kl_vecs.shape
    kept = 2 * share
    channels, modes, entries = weights.shape[1:]
    deep = channels * modes
    half = reals // 2
    parts = 6
    dma = pltpu.SemaphoreType.DMA
    return pl.pallas_call(
        functools.partial(project_kernel, size),
        out_shape=jax.ShapeDtypeStruct((slots, kept, half), jnp.bfloat16),
        in_specs=[pl.BlockSpec(memory_space=pl.ANY)] * 3,
        out_specs=pl.BlockSpec(memory_space=pl.ANY),
        scratch_shapes=[
            pltpu.VMEM((reals, LANES), jnp.int32),
            pltpu.VMEM((reals, entries), jnp.int32),
            pltpu.VMEM((size, channels, modes, entries), jnp.bfloat16),
            pltpu.VMEM((size + 1, kept, deep), jnp.bfloat16),
            pltpu.VMEM((2, reals, deep), jnp.bfloat16),
            pltpu.VMEM((kept, reals), jnp.float32),
            pltpu.VMEM((kept, half), jnp.bfloat16),
            pltpu.VMEM((kept, half), jnp.bfloat16),
            dma((3,)),
            dma((size,)),
            dma((size,)),
            dma((size,)),
            dma((size,)),
            dma((size,)),
            dma((parts,)),
            dma((parts,)),
            dma((parts,)),
        ],
        compiler_params=pltpu.CompilerParams(
            collective_id=0, has_side_effects=True, vmem_limit_bytes=60 * 2**20
        ),
        name="project",
    )(base, weights, kl_vecs)


def per_device(seeds, noise_amp, singular_projection, kl_vecs, m_order, mode_counts):
    size = lax.axis_size("freq")
    z = lax.axis_index("freq")
    c = lax.axis_index("mgrp")
    slots, share, _ = kl_vecs.shape
    half = seeds.shape[1]

    ahead = (z + jnp.arange(size, dtype=jnp.int32)) % size
    picked = m_order[ahead * slots + c]
    amp = (noise_amp * (1.0 / 18918.0))[:, None, :]
    weights = weigh(picked, singular_projection, amp)

    mine = m_order[z * slots + (c + jnp.arange(slots, dtype=jnp.int32)) % slots]
    steps = jnp.arange(LANES, dtype=jnp.int32) * GOLDEN
    base = seeds[mine][:, :, None] + steps[None, None, :]

    coeffs = project(size, base, weights, kl_vecs, 2 * half)
    limits = mode_counts[m_order[z * slots + jnp.arange(slots, dtype=jnp.int32)]]
    row_index = jnp.arange(2 * share, dtype=jnp.int32)
    return jnp.where(row_index[None, :, None] < limits[:, None, None], coeffs, jnp.bfloat16(0))


def solution(mesh):
    placed = (
        P("groups", "mgrp"),
        P(("groups", "freq"), None),
        P("groups", "freq", None, None),
        P(("groups", "freq"), "mgrp", None),
        P("groups"),
        P("groups"),
    )
    return jax.shard_map(
        per_device,
        mesh=mesh,
        in_specs=placed,
        out_specs=P(("groups", "freq"), None, "mgrp"),
        check_vma=False,
    )
```

time: 577 us -> 271 us (0.47)
  matrix products: 268 us -> 0 us
  Pallas kernels: 0 us -> 260 us
  waiting for transfers between devices: 189 us -> 0 us
  local copies, waits for them, and re-layouts: 68.1 us -> 5.63 us
  starting transfers between devices: 29.2 us -> 0 us
  between operations: 13.5 us -> 0.06 us
    dot_general x10 -> x0, matrix products: 268 us -> none  [the longest x8 245 us: project(): jnp.einsum('fkb,fbr->fkr', weights, visible, preferred_element_type=jnp.f...]
    pallas_call x0 -> x2, Pallas kernels: none -> 260 us  [the longest x1 249 us: project(): pl.pallas_call(functools.partial(project_kernel, size), out_shape=jax.Sha...]
    all_to_all x2 -> x0, waiting for transfers between devices: 168 us -> none  [per_device(): lax.all_to_all(outgoing, 'freq', split_axis=0, concat_axis=1, tiled=True)]
    gather x16 -> x5, local copies, waits for them, and re-layouts: 40 us -> 4.99 us  [the longest x1 1.86 us: per_device(): picked = m_order[ahead * slots + c]]
    all_to_all x2 -> x0, starting transfers between devices: 28.9 us -> none  [per_device(): lax.all_to_all(outgoing, 'freq', split_axis=0, concat_axis=1, tiled=True)]
    all_gather x2 -> x0, waiting for transfers between devices: 20.2 us -> none  [per_device(): lax.all_gather(eigen_panel, 'mgrp', axis=0, tiled=True)]
    slice x2 -> x0, local copies, waits for them, and re-layouts: 11.2 us -> none  [the longest x1 10.5 us: per_device(): eigen_panel = kl_vecs[batch_index]]
    dynamic_update_slice x8 -> x0, local copies, waits for them, and re-layouts: 8.55 us -> none  [per_device(): grouped = lax.map(jax.vmap(project), m_numbers.reshape(-1, 4))]
  transfers between devices with their start and end apart: 4 -> 0, of which waited for: 3 -> 0; matrix products, arithmetic and copies ran while one was open for 30% -> 0% of each run, Pallas kernels for 0% -> 0%
where the time goes in v1:
time: 271 us
  Pallas kernels  260 us (96%)
  local copies, waits for them, and re-layouts  5.63 us (2%)
  other arithmetic  5.27 us (2%)
    pallas_call x1, Pallas kernels, project(): pl.pallas_call(functools.partial(project_kernel, size), out_shape=jax.Sha...  249 us
    pallas_call x1, Pallas kernels, weigh(): pl.pallas_call(weigh_kernel, out_shape=jax.ShapeDtypeStruct((count,) + pr...  11 us

profile of v1, /device:TPU:69, one launch (start us, length us, event | category | flops | bytes accessed | tf_op | source)
XLA Modules:
  0.0 270.6 jit_solution(6388231111315616134)
XLA Ops:
  0.0 0.0 copy-start
  0.0 1.3 gather_fusion.2
  1.3 0.0 copy-done
  1.3 0.6 gather_fusion.3
  1.9 1.0 broadcast_add_fusion.base_ref
  2.9 1.9 gather_fusion.4
  4.8 0.8 broadcast_multiply_fusion
  5.6 0.6 broadcast_in_dim.11.amp
  6.2 11.0 %weigh.1.weights_ref = bf16[16,16,16,512]{3,2,1,0:T(8,128)(2,1)} custom-call(s32[16]{0:T(128)} %gather_fusion.4, bf16[32,16,16,512]{3,2,1,0:T(8,128)(2,1)} %projection.1, f32[16,1,512]{2,1,0:T(1,128)} %broadcast_in_dim.11.amp), custom_call_target="tpu_custom_call" | custom-call | tf_op jit(solution)/shard_map/weigh/pallas_call | solution.py:41
  17.2 0.0 copy-start.1
  17.2 0.0 copy-start.2
  17.2 248.7 %project.1 = bf16[2,1536,512]{2,1,0:T(8,128)(2,1)} custom-call(s32[2,512,128]{2,1,0:T(8,128)} %broadcast_add_fusion.base_ref, bf16[16,16,16,512]{3,2,1,0:T(8,128)(2,1)} %weigh.1.weights_ref, bf16[2,768,4096]{2,1,0:T(8,128)(2,1)} %kl_ref.1), custom_call_target="tpu_custom_call" | custom-call | tf_op jit(solution)/shard_map/project/pallas_call | solution.py:239
  265.9 0.0 copy-done.1
  265.9 0.6 gather_fusion
  266.5 0.0 copy-done.2
  266.6 0.6 gather_fusion.1
  267.2 0.1 iota_compare_fusion
  267.3 3.4 %broadcast_select_fusion = bf16[2,1536,512]{2,1,0:T(8,128)(2,1)} fusion(bf16[2,1536,512]{2,1,0:T(8,128)(2,1)} %project.1, pred[2,1536]{1,0:T(4,128)(4,1)S(1)} %iota_compare_fusion), kind=kLoop, calls=%fused_computation.5 | loop fusion | flops 1572864 | bytes 6294528 | tf_op jit(solution)/shard_map/jit(_where)/select_n | solution.py:289
  (10 shorter events, 0.1 us)
Async XLA Ops:
  0.0 1.3 copy-start
  17.2 248.7 %copy-start.1 = (s32[32]{0:T(128)S(1)}, s32[32]{0:T(128)}, u32[]{:S(2)}) copy-start(s32[32]{0:T(128)} %param.10) | copy-start | bytes 388
  17.2 249.4 %copy-start.2 = (s32[32]{0:T(128)S(1)}, s32[32]{0:T(128)}, u32[]{:S(2)}) copy-start(s32[32]{0:T(128)} %param.11) | copy-start | bytes 388

commit v2 on v1

--- a/solution.py
+++ b/solution.py
@@ -14,6 +14,8 @@
 MESH = pl.DeviceIdType.MESH
 LANES = 128
 ROWS = 128
+GATHERED = 4
+CENTRE = 32767.5
 NT = (((1,), (1,)), ((), ()))
 
 
@@ -27,31 +29,40 @@
     x = x ^ lax.shift_right_logical(x, 15)
     x = x * MIX_B
     x = x ^ lax.shift_right_logical(x, 16)
-    return ((x & 65535).astype(jnp.float32) - 32767.5).astype(jnp.bfloat16)
-
-
-def weigh_kernel(picked, projection, amp, out):
-    del picked
-    out[0] = (projection[0].astype(jnp.float32) * amp[...]).astype(jnp.bfloat16)
-
-
-def weigh(picked, projection, amp):
-    count = picked.shape[0]
+    return (x & 65535).astype(jnp.float32).astype(jnp.bfloat16)
+
+
+def weigh_kernel(order, place, *refs):
+    del order, place
+    *projections, amp, out = refs
+    for i, projection in enumerate(projections):
+        for f in range(amp.shape[0]):
+            level = amp[f:f + 1, :] * (1.0 / 18918.0)
+            out[i, f] = (projection[0, f].astype(jnp.float32) * level).astype(jnp.bfloat16)
+
+
+def weigh(order, place, size, slots, projection, amp):
     block = (1,) + projection.shape[1:]
+
+    def pick(i):
+        def index(d, order, place):
+            chip = lax.rem(place[0] + d * GATHERED + i, size)
+            return order[chip * slots + place[1]], 0, 0, 0
+
+        return index
+
     return pl.pallas_call(
         weigh_kernel,
-        out_shape=jax.ShapeDtypeStruct((count,) + projection.shape[1:], jnp.bfloat16),
+        out_shape=jax.ShapeDtypeStruct((size,) + projection.shape[1:], jnp.bfloat16),
         grid_spec=pltpu.PrefetchScalarGridSpec(
-            num_scalar_prefetch=1,
-            grid=(count,),
-            in_specs=[
-                pl.BlockSpec(block, lambda d, picked: (picked[d], 0, 0, 0)),
-                pl.BlockSpec(amp.shape, lambda d, picked: (0, 0, 0)),
-            ],
-            out_specs=pl.BlockSpec(block, lambda d, picked: (d, 0, 0, 0)),
+            num_scalar_prefetch=2,
+            grid=(size // GATHERED,),
+            in_specs=[pl.BlockSpec(block, pick(i)) for i in range(GATHERED)]
+            + [pl.BlockSpec(amp.shape, lambda d, order, place: (0, 0))],
+            out_specs=pl.BlockSpec((GATHERED,) + projection.shape[1:], lambda d, order, place: (d, 0, 0, 0)),
         ),
         name="weigh",
-    )(picked, projection, amp)
+    )(order, place, *[projection] * GATHERED, amp)
 
 
 def project_kernel(
@@ -161,6 +172,9 @@
                 after = [jnp.zeros((LANES - (u + 1) * modes, entries), jnp.bfloat16)] if u + 1 < per_trip else []
                 rows.append(jnp.concatenate(before + [weights[at, t * per_trip + u]] + after, 0))
             stacked = jnp.concatenate(rows, 1)
+            ones = jnp.ones((16, per_trip * entries), jnp.bfloat16)
+            total = lax.dot_general(ones, stacked, NT, preferred_element_type=jnp.float32)
+            shift = total[0:1, :] * CENTRE
             top = pl.multiple_of(t * slab, slab)
             blocks = reals // ROWS
             wide_n = 2 * ROWS
@@ -178,7 +192,7 @@
                     ],
                     1,
                 )
-                projected = lax.dot_general(visible, stacked, NT, preferred_element_type=jnp.float32)
+                projected = lax.dot_general(visible, stacked, NT, preferred_element_type=jnp.float32) - shift
                 svd[cur, here, pl.ds(pl.multiple_of(t * LANES, LANES), LANES)] = projected.astype(jnp.bfloat16)
 
     local_panel(source(size - 1)).wait()
@@ -274,17 +288,16 @@
     slots, share, _ = kl_vecs.shape
     half = seeds.shape[1]
 
-    ahead = (z + jnp.arange(size, dtype=jnp.int32)) % size
-    picked = m_order[ahead * slots + c]
-    amp = (noise_amp * (1.0 / 18918.0))[:, None, :]
-    weights = weigh(picked, singular_projection, amp)
+    place = jnp.stack([z, c]).astype(jnp.int32)
+    weights = weigh(m_order, place, size, slots, singular_projection, noise_amp)
 
     mine = m_order[z * slots + (c + jnp.arange(slots, dtype=jnp.int32)) % slots]
     steps = jnp.arange(LANES, dtype=jnp.int32) * GOLDEN
     base = seeds[mine][:, :, None] + steps[None, None, :]
 
     coeffs = project(size, base, weights, kl_vecs, 2 * half)
-    limits = mode_counts[m_order[z * slots + jnp.arange(slots, dtype=jnp.int32)]]
+    limits = mode_counts[mine]
+    limits = jnp.where(c == 0, limits, limits[::-1])
     row_index = jnp.arange(2 * share, dtype=jnp.int32)
     return jnp.where(row_index[None, :, None] < limits[:, None, None], coeffs, jnp.bfloat16(0))
 

time: 271 us -> 258 us (0.952)
  Pallas kernels: 260 us -> 250 us
  local copies, waits for them, and re-layouts: 5.63 us -> 2.6 us
    pallas_call x1, Pallas kernels: 11 us -> 5.64 us  [weigh(): pl.pallas_call(weigh_kernel, out_shape=jax.ShapeDtypeStruct((size,) + pro...]
    pallas_call x1, Pallas kernels: 249 us -> 245 us  [project(): pl.pallas_call(functools.partial(project_kernel, size), out_shape=jax.Sha...]
where the time goes in v2:
time: 258 us
  Pallas kernels  250 us (97%)
  other arithmetic  5.14 us (2%)
  local copies, waits for them, and re-layouts  2.6 us (1%)
    pallas_call x1, Pallas kernels, project(): pl.pallas_call(functools.partial(project_kernel, size), out_shape=jax.Sha...  245 us
    pallas_call x1, Pallas kernels, weigh(): pl.pallas_call(weigh_kernel, out_shape=jax.ShapeDtypeStruct((size,) + pro...  5.64 us

profile of v2, /device:TPU:69, one launch (start us, length us, event | category | flops | bytes accessed | tf_op | source)
XLA Modules:
  0.0 258.2 jit_solution(15188184946095642425)
XLA Ops:
  0.0 0.0 copy-start
  0.0 1.3 gather_fusion
  1.3 0.0 copy-done
  1.4 0.6 gather_fusion.2
  1.9 1.0 broadcast_add_fusion.base_ref
  2.9 0.7 pad_add_fusion.place
  3.6 5.6 %weigh.1.weights_ref = bf16[16,16,16,512]{3,2,1,0:T(8,128)(2,1)} custom-call(s32[32]{0:T(128)} %order.1, s32[2]{0:T(128)} %pad_add_fusion.place, bf16[32,16,16,512]{3,2,1,0:T(8,128)(2,1)} %refs_3_.1, bf16[32,16,16,512]{3,2,1,0:T(8,128)(2,1)} %refs_3_.1, bf16[32,16,16,512]{3,2,1,0:T(8,128)(2,1)} %refs_3_.1, bf16[32,16,16,512]{3,2,1,0:T(8,128)(2,1)} %refs_3_.1, ...), custom_call_target="tpu_custom_call" | custom-call | tf_op jit(solution)/shard_map/weigh/pallas_call | solution.py:54
  9.2 0.0 copy-start.1
  9.2 244.8 %project.1 = bf16[2,1536,512]{2,1,0:T(8,128)(2,1)} custom-call(s32[2,512,128]{2,1,0:T(8,128)} %broadcast_add_fusion.base_ref, bf16[16,16,16,512]{3,2,1,0:T(8,128)(2,1)} %weigh.1.weights_ref, bf16[2,768,4096]{2,1,0:T(8,128)(2,1)} %kl_ref.1), custom_call_target="tpu_custom_call" | custom-call | tf_op jit(solution)/shard_map/project/pallas_call | solution.py:253
  254.0 0.0 copy-done.1
  254.1 0.6 gather_fusion.1
  254.7 0.1 rev.3
  254.8 0.1 iota_compare_fusion
  254.9 3.4 %broadcast_select_fusion = bf16[2,1536,512]{2,1,0:T(8,128)(2,1)} fusion(bf16[2,1536,512]{2,1,0:T(8,128)(2,1)} %project.1, pred[2,1536]{1,0:T(4,128)(4,1)S(1)} %iota_compare_fusion), kind=kLoop, calls=%fused_computation.3 | loop fusion | flops 1572864 | bytes 6294528 | tf_op jit(solution)/shard_map/jit(_where)/select_n | solution.py:302
  (6 shorter events, 0.0 us)
Async XLA Ops:
  0.0 1.3 copy-start
  9.2 244.8 %copy-start.1 = (s32[32]{0:T(128)S(1)}, s32[32]{0:T(128)}, u32[]{:S(2)}) copy-start(s32[32]{0:T(128)} %param.11) | copy-start | bytes 388
